TPU v7x, 256 devices: a whole 4x4x8 slice. The times are simulated.
256 devices in a mesh: gx: 16 (over z_lo, x), gy: 4 (over y), gz: 4 (over z_hi, core).
Axes of the slice: x: 4, y: 4, z: 8 (z_hi: 2, z_lo: 4; z = z_hi * 4 + z_lo), core: 2. Of those that a mesh axis runs over, the one named last changes fastest.
Arguments:
- displacement: float32 [3, 128, 32, 512], P(None, 'gx', 'gz', 'gy'), may hold values from -0.1 to 0.1
- velocity: float32 [3, 128, 32, 512], P(None, 'gx', 'gz', 'gy'), may hold values from -0.4 to 0.4
- body_force: float32 [3, 128, 32, 512], P(None, 'gx', 'gz', 'gy'), may hold values from -4 to 4
- broken: int32 [12, 128, 32, 512], P(None, 'gx', 'gz', 'gy'), may hold values from 0 to 1073741823
Outputs:
- new_displacement: float32 [3, 128, 32, 512], P(None, 'gx', 'gz', 'gy')
- new_velocity: float32 [3, 128, 32, 512], P(None, 'gx', 'gz', 'gy')
- new_acceleration: float32 [3, 128, 32, 512], P(None, 'gx', 'gz', 'gy')
- strain_energy: float32 [], replicated
All inputs are finite; a program needn't handle non-finite values.
Results may differ from a plain program's by a relative error of at most 0.0003.
Values sent between devices are 32-bit elements; how exact they have to be, the bound alone decides.
A program may use at most 128 MiB of HBM per device.

v0:
```python
import functools
import math

import jax
import jax.numpy as jnp
from jax import lax
from jax.experimental import pallas as pl
from jax.experimental.pallas import tpu as pltpu
from jax.sharding import PartitionSpec as P

MESH = pl.DeviceIdType.MESH
TIME_STEP = 0.05
BITS_PER_WORD = 30
SIDE_X = 4
R = 3
NB = 8
EXT = NB + 2 * R
LANES = 128
REACH = range(-R, R + 1)

FAR = [
    (ez, ex, ey) for ez in (-1, 1) for ex in (0, -1, 1) for ey in (0, -1, 1)
]
NEAR = [(0, ex, ey) for ex in (0, -1, 1) for ey in (0, -1, 1) if (ex, ey) != (0, 0)]
SOURCES = FAR + NEAR
SLOT = {e: i for i, e in enumerate(SOURCES)}

CLASSES = {}
for _p in REACH:
    for _r in REACH:
        CLASSES.setdefault(_p * _p + _r * _r, []).append((_p, _r))
CLASSES = sorted(CLASSES.items())


def side(e):
    return 0 if e < 0 else 1


def bond_number(p, q, r):
    flat = (p + R) * 49 + (q + R) * 7 + (r + R)
    return flat if flat < 171 else flat - 1


def weight(p, q, r):
    return 4.0 * math.exp(-(p * p + q * q + r * r) / 9.0)


def kernel(
    sizes,
    disp,
    vel,
    body,
    broken,
    newd_out,
    newv_out,
    newa_out,
    energy_out,
    core,
    xpack,
    ypack,
    zrecv,
    xrecv,
    zxrecv,
    yrecv,
    yext,
    ext,
    bonds,
    force,
    esum,
    erow,
    eplane,
    ecol,
    send_sem,
    recv_sem,
    esend_sem,
    erecv_sem,
):
    n_gx, n_gy, n_gz = sizes
    gx, gy, gz = lax.axis_index("gx"), lax.axis_index("gy"), lax.axis_index("gz")
    has_low, has_high = gz > 0, gz < n_gz - 1

    def at(ez, ex, ey):
        return (
            lax.rem(gx + ex + n_gx, n_gx),
            lax.rem(gy + ey + n_gy, n_gy),
            gz + ez,
        )

    side_x = SIDE_X
    n_plane = side_x * n_gy * 2
    n_col = (n_gx // side_x) * (n_gz // 2)
    my_x, my_zlo = lax.rem(gx, side_x), gx // side_x
    my_core, my_zhi = lax.rem(gz, 2), gz // 2
    my_plane = (my_x * n_gy + gy) * 2 + my_core
    my_col = my_zhi * (n_gx // side_x) + my_zlo

    def plane_device(m):
        return (
            my_zlo * side_x + m // (2 * n_gy),
            lax.rem(m // 2, n_gy),
            my_zhi * 2 + lax.rem(m, 2),
        )

    def col_device(m):
        return (
            lax.rem(m, n_gx // side_x) * side_x + my_x,
            gy,
            (m // (n_gx // side_x)) * 2 + my_core,
        )

    barrier = pltpu.get_barrier_semaphore()

    def greet(device):
        pl.semaphore_signal(barrier, inc=1, device_id=device, device_id_type=MESH)

    for present, low in ((has_low, True), (has_high, False)):

        @pl.when(present)
        def _(low=low):
            for e in FAR:
                if (e[0] < 0) == low:
                    greet(at(*e))

    for e in NEAR:
        greet(at(*e))

    @pl.loop(1, n_plane)
    def _(j):
        greet(plane_device(lax.rem(my_plane + j, n_plane)))

    @pl.loop(1, n_col)
    def _(j):
        greet(col_device(lax.rem(my_col + j, n_col)))

    lane = lax.broadcasted_iota(jnp.int32, (NB, LANES), 1)
    lane2 = lax.broadcasted_iota(jnp.int32, (2 * NB, LANES), 1)

    for present, low in ((has_low, True), (has_high, False)):

        @pl.when(jnp.logical_not(present))
        def _(low=low):
            s = 0 if low else 1
            for step in (0, 1):
                zrecv[step, s] = jnp.zeros(zrecv.shape[2:], jnp.float32)
                zxrecv[step, s] = jnp.zeros(zxrecv.shape[2:], jnp.float32)
                for e in FAR:
                    if (e[0] < 0) == low and e[2] != 0:
                        yrecv[step, SLOT[e]] = jnp.zeros((NB, LANES), jnp.float32)

    def message(step, e):
        ez, ex, ey = e
        slot = SLOT[e]
        if ey != 0:
            src, dst = ypack.at[step, side(ey)], yrecv.at[step, slot]
        elif ex == 0:
            src = core.at[step, pl.ds(NB - R if ez < 0 else 0, R)]
            dst = zrecv.at[step, side(ez)]
        elif ez == 0:
            src, dst = xpack.at[step, side(ex)], xrecv.at[step, side(ex)]
        else:
            src = xpack.at[step, side(ex), pl.ds(40 if ez < 0 else 0, 32)]
            dst = zxrecv.at[step, side(ez), side(ex)]
        return pltpu.make_async_remote_copy(
            src_ref=src,
            dst_ref=dst,
            send_sem=send_sem.at[step, slot],
            recv_sem=recv_sem.at[step, slot],
            device_id=at(-ez, -ex, -ey),
            device_id_type=MESH,
        )

    def send(step):
        for present, up in ((has_high, True), (has_low, False)):

            @pl.when(present)
            def _(up=up):
                for e in FAR:
                    if (e[0] < 0) == up:
                        message(step, e).start()

        for e in NEAR:
            message(step, e).start()

    def receive_far(step):
        for present, low in ((has_low, True), (has_high, False)):

            @pl.when(present)
            def _(low=low):
                for e in FAR:
                    if (e[0] < 0) == low:
                        message(step, e).wait_recv()

    def finish_sends(step):
        for present, up in ((has_high, True), (has_low, False)):

            @pl.when(present)
            def _(up=up):
                for e in FAR:
                    if (e[0] < 0) == up:
                        message(step, e).wait_send()

        for e in NEAR:
            message(step, e).wait_send()

    def pack(step):
        ylow = jnp.zeros((NB, LANES), jnp.float32)
        yhigh = jnp.zeros((NB, LANES), jnp.float32)
        for z in range(NB):
            for c in range(3):
                g = 3 * (z * 3 + c)
                value = core[step, z, c]
                ext[R, z + R, c, R : R + NB, :] = value
                xpack[step, 0, g : g + R, :] = core[step, z, c, NB - R : NB, :]
                xpack[step, 1, g : g + R, :] = core[step, z, c, 0:R, :]
                mine = (lane >= g) & (lane < g + R)
                ylow = jnp.where(mine, pltpu.roll(value, (g + R) % LANES, 1), ylow)
                yhigh = jnp.where(mine, pltpu.roll(value, g, 1) if g else value, yhigh)
        ypack[step, 0] = ylow
        ypack[step, 1] = yhigh

    def fill_rows(step, ez):
        first, count, base = (
            (0, R, NB - R) if ez < 0 else (R, NB, 0) if ez == 0 else (R + NB, R, 0)
        )
        lead = 40 if ez < 0 else 0
        for i in range(count):
            for c in range(3):
                g = 3 * ((base + i) * 3 + c) - lead
                if ez != 0:
                    ext[R, first + i, c, R : R + NB, :] = zrecv[step, side(ez), i, c]
                for s, row in ((0, 0), (1, R + NB)):
                    if ez == 0:
                        strip = xrecv[step, s, g : g + R, :]
                    else:
                        strip = zxrecv[step, side(ez), s, g : g + R, :]
                    ext[R, first + i, c, row : row + R, :] = strip
        for s, ey in ((0, -1), (1, 1)):
            yext[s, R : R + NB, :] = yrecv[step, SLOT[(ez, 0, ey)]]
            yext[s, 0:R, :] = yrecv[step, SLOT[(ez, -1, ey)], NB - R : NB, :]
            yext[s, R + NB : EXT, :] = yrecv[step, SLOT[(ez, 1, ey)], 0:R, :]

        @pl.loop(0, count)
        def _(i):
            for c in range(3):
                g = 3 * ((base + i) * 3 + c)
                left = pltpu.roll(yext[0], lax.rem(2 * LANES - R - g, LANES), 1)
                right = pltpu.roll(yext[1], lax.rem(LANES - g, LANES), 1)
                here = ext[R, first + i, c]
                for r in range(1, R + 1):
                    ext[R + r, first + i, c] = pltpu.roll(
                        jnp.where(lane2 < r, right, here), LANES - r, 1
                    )
                    ext[R - r, first + i, c] = pltpu.roll(
                        jnp.where(lane2 >= LANES - r, left, here), r, 1
                    )

    def unpack_bonds():
        @pl.loop(0, NB)
        def _(z):
            words = [broken[w, pl.ds(z, NB, stride=NB), :] for w in range(12)]
            depth = gz * NB + z
            for q in REACH:
                inside = (depth + q >= 0) & (depth + q < n_gz * NB)
                scale = jnp.where(inside, 1.0, 0.0)
                for _, members in CLASSES:
                    whole = jnp.full(
                        (NB, LANES), scale * weight(members[0][0], q, members[0][1])
                    )
                    for p, r in members:
                        j = (p + R) * 7 + r + R
                        if (p, q, r) == (0, 0, 0):
                            bonds[z, q + R, j] = jnp.zeros((NB, LANES), jnp.float32)
                            continue
                        k = bond_number(p, q, r)
                        bit = words[k // BITS_PER_WORD] & (1 << (k % BITS_PER_WORD))
                        bonds[z, q + R, j] = jnp.where(bit == 0, whole, 0.0)

    def add_row(step, z, q, with_energy):
        cx, cz, cy = (core[step, z, c] for c in range(3))
        cz = cz - q.astype(jnp.float32)
        cxs = {p: cx - float(p) if p else cx for p in REACH}
        cys = {r: cy - float(r) if r else cy for r in REACH}
        row = z + q + R
        fx = fz = fy = energy = None

        def plus(a, b):
            return b if a is None else a + b

        for square, members in CLASSES:
            own = jnp.where(q == 0, 1, 0) if square == 0 else 0
            rest_square = (q * q + square + own).astype(jnp.float32)
            inverse_rest = lax.rsqrt(jnp.full((NB, LANES), rest_square))
            class_energy = None
            for p, r in members:
                there = ext.at[r + R, row]
                bx = there[0, R + p : R + p + NB, :] - cxs[p]
                bz = there[1, R + p : R + p + NB, :] - cz
                by = there[2, R + p : R + p + NB, :] - cys[r]
                length_square = bx * bx + bz * bz + by * by
                if square == 0:
                    length_square = length_square + own.astype(jnp.float32)
                gap = inverse_rest - lax.rsqrt(length_square)
                pull = bonds[z, q + R, (p + R) * 7 + r + R] * gap
                fx = plus(fx, pull * bx)
                fz = plus(fz, pull * bz)
                fy = plus(fy, pull * by)
                if with_energy:
                    class_energy = plus(class_energy, pull * gap * length_square)
            if with_energy:
                rest = jnp.full((NB, LANES), rest_square) * inverse_rest
                energy = plus(energy, class_energy * rest)
        force[step, z, 0] += fx
        force[step, z, 1] += fz
        force[step, z, 2] += fy
        if with_energy:
            esum[...] += energy

    def add_pair(step, z, q, with_energy):
        add_row(step, z, q, with_energy)
        add_row(step, NB - 1 - z, -q, with_energy)

    def inner_rows(step, with_energy):
        @pl.loop(0, R + 1)
        def _(q):
            @pl.loop(0, jnp.where(q == 0, NB // 2, NB - q))
            def _(z):
                add_pair(step, z, q, with_energy)

    def outer_rows(step, with_energy):
        @pl.loop(1, R + 1)
        def _(q):
            @pl.loop(NB - q, NB)
            def _(z):
                add_pair(step, z, q, with_energy)

    def exchange_and_sum(step, with_energy, between):
        pack(step)
        if step == 0:
            greeted = (
                len(NEAR)
                + (len(FAR) // 2)
                * (jnp.where(has_low, 1, 0) + jnp.where(has_high, 1, 0))
                + n_plane
                - 1
                + n_col
                - 1
            )
            pl.semaphore_wait(barrier, greeted)
        send(step)
        between()
        for e in NEAR:
            message(step, e).wait_recv()
        fill_rows(step, 0)
        inner_rows(step, with_energy)
        receive_far(step)
        fill_rows(step, -1)
        fill_rows(step, 1)
        outer_rows(step, with_energy)

    def start_force(step):
        @pl.loop(0, NB)
        def _(z):
            for c in range(3):
                force[step, z, c] = body[c, pl.ds(z, NB, stride=NB), :]

    def before_first():
        unpack_bonds()
        start_force(0)

    @pl.loop(0, NB)
    def _(z):
        for c in range(3):
            core[0, z, c] = disp[c, pl.ds(z, NB, stride=NB), :]

    exchange_and_sum(0, False, before_first)

    @pl.loop(0, NB)
    def _(z):
        for c in range(3):
            rows = pl.ds(z, NB, stride=NB)
            moved = (
                core[0, z, c]
                + TIME_STEP * vel[c, rows, :]
                + (0.5 * TIME_STEP * TIME_STEP) * force[0, z, c]
            )
            core[1, z, c] = moved
            newd_out[c, rows, :] = moved

    esum[...] = jnp.zeros((NB, LANES), jnp.float32)
    exchange_and_sum(1, True, lambda: start_force(1))

    erow[0] = jnp.sum(esum[...], axis=0, keepdims=True)
    eplane[my_plane] = erow[0]

    def plane_message(j, slot, device):
        return pltpu.make_async_remote_copy(
            src_ref=erow.at[0],
            dst_ref=eplane.at[slot],
            send_sem=esend_sem.at[0, j],
            recv_sem=erecv_sem.at[0, j],
            device_id=plane_device(device),
            device_id_type=MESH,
        )

    @pl.loop(1, n_plane)
    def _(j):
        plane_message(j, my_plane, lax.rem(my_plane + j, n_plane)).start()

    @pl.loop(0, NB)
    def _(z):
        for c in range(3):
            rows = pl.ds(z, NB, stride=NB)
            newa = force[1, z, c]
            newa_out[c, rows, :] = newa
            newv_out[c, rows, :] = vel[c, rows, :] + (0.5 * TIME_STEP) * (
                force[0, z, c] + newa
            )

    finish_sends(0)
    finish_sends(1)

    @pl.loop(1, n_plane)
    def _(j):
        other = lax.rem(my_plane - j + n_plane, n_plane)
        plane_message(j, other, other).wait()

    total = eplane[0]
    for m in range(1, n_plane):
        total = total + eplane[m]
    erow[1] = total
    ecol[my_col] = total

    def col_message(j, slot, device):
        return pltpu.make_async_remote_copy(
            src_ref=erow.at[1],
            dst_ref=ecol.at[slot],
            send_sem=esend_sem.at[1, j],
            recv_sem=erecv_sem.at[1, j],
            device_id=col_device(device),
            device_id_type=MESH,
        )

    @pl.loop(1, n_col)
    def _(j):
        col_message(j, my_col, lax.rem(my_col + j, n_col)).start()

    @pl.loop(1, n_col)
    def _(j):
        other = lax.rem(my_col - j + n_col, n_col)
        col_message(j, other, other).wait()

    total = ecol[0]
    for m in range(1, n_col):
        total = total + ecol[m]
    area = (n_gx * NB) * (n_gy * LANES)
    energy_out[0, 0] = jnp.sum(total) * (0.25 / area)


def solution(mesh):
    sizes = (mesh.shape["gx"], mesh.shape["gy"], mesh.shape["gz"])
    f32 = jnp.float32
    block = jax.ShapeDtypeStruct((3, NB * NB, LANES), f32)

    def step(displacement, velocity, body_force, broken):
        flat = [
            a.reshape(a.shape[0], NB * NB, LANES)
            for a in (displacement, velocity, body_force, broken)
        ]
        newd, newv, newa, energy = pl.pallas_call(
            functools.partial(kernel, sizes),
            out_shape=(block, block, block, jax.ShapeDtypeStruct((1, 1), f32)),
            in_specs=[pl.BlockSpec(memory_space=pltpu.VMEM)] * 4,
            out_specs=[pl.BlockSpec(memory_space=pltpu.VMEM)] * 3
            + [pl.BlockSpec(memory_space=pltpu.SMEM)],
            scratch_shapes=[
                pltpu.VMEM((2, NB, 3, NB, LANES), f32),
                pltpu.VMEM((2, 2, 72, LANES), f32),
                pltpu.VMEM((2, 2, NB, LANES), f32),
                pltpu.VMEM((2, 2, R, 3, NB, LANES), f32),
                pltpu.VMEM((2, 2, 72, LANES), f32),
                pltpu.VMEM((2, 2, 2, 32, LANES), f32),
                pltpu.VMEM((2, len(SOURCES), NB, LANES), f32),
                pltpu.VMEM((2, 2 * NB, LANES), f32),
                pltpu.VMEM((7, EXT, 3, 2 * NB, LANES), f32),
                pltpu.VMEM((NB, 7, 49, NB, LANES), f32),
                pltpu.VMEM((2, NB, 3, NB, LANES), f32),
                pltpu.VMEM((NB, LANES), f32),
                pltpu.VMEM((2, 1, LANES), f32),
                pltpu.VMEM((32, 1, LANES), f32),
                pltpu.VMEM((8, 1, LANES), f32),
                pltpu.SemaphoreType.DMA((2, len(SOURCES))),
                pltpu.SemaphoreType.DMA((2, len(SOURCES))),
                pltpu.SemaphoreType.DMA((2, 32)),
                pltpu.SemaphoreType.DMA((2, 32)),
            ],
            compiler_params=pltpu.CompilerParams(
                collective_id=0,
                has_side_effects=True,
                vmem_limit_bytes=40 * 1024 * 1024,
            ),
        )(*flat)
        shape = displacement.shape
        return (
            newd.reshape(shape),
            newv.reshape(shape),
            newa.reshape(shape),
            energy.reshape(()),
        )

    spec = P(None, "gx", "gz", "gy")
    return jax.shard_map(
        step,
        mesh=mesh,
        in_specs=(spec,) * 4,
        out_specs=(spec,) * 3 + (P(),),
        check_vma=False,
    )
```

profile of v0, /device:TPU:1, one launch (start us, length us, event | category | flops | bytes accessed | tf_op | source)
XLA Modules:
  0.0 66.1 jit_solution(8823905916184667223)
XLA Ops:
  0.6 0.0 copy-start
  0.6 1.0 %copy-done = s32[12,8,8,128]{3,2,1,0:T(8,128)S(1)} copy-done((s32[12,8,8,128]{3,2,1,0:T(8,128)S(1)}, s32[12,8,8,128]{3,2,1,0:T(8,128)}, u32[]{:S(2)}) %copy-start) | copy-done | bytes 393240
  1.6 0.0 copy-start.1
  1.6 0.9 %copy-done.1 = f32[3,8,8,128]{3,2,1,0:T(8,128)S(1)} copy-done((f32[3,8,8,128]{3,2,1,0:T(8,128)S(1)}, f32[3,8,8,128]{3,2,1,0:T(8,128)}, u32[]{:S(2)}) %copy-start.1) | copy-done | bytes 98328
  2.5 0.0 copy-start.2
  2.5 0.9 %copy-done.2 = f32[3,8,8,128]{3,2,1,0:T(8,128)S(1)} copy-done((f32[3,8,8,128]{3,2,1,0:T(8,128)S(1)}, f32[3,8,8,128]{3,2,1,0:T(8,128)}, u32[]{:S(2)}) %copy-start.2) | copy-done | bytes 98328
  3.4 0.0 copy-start.3
  3.4 0.9 %copy-done.3 = f32[3,8,8,128]{3,2,1,0:T(8,128)S(1)} copy-done((f32[3,8,8,128]{3,2,1,0:T(8,128)S(1)}, f32[3,8,8,128]{3,2,1,0:T(8,128)}, u32[]{:S(2)}) %copy-start.3) | copy-done | bytes 98328
  4.3 58.1 %shard_map.75 = (f32[3,64,128]{2,1,0:T(8,128)S(1)}, f32[3,64,128]{2,1,0:T(8,128)S(1)}, f32[3,64,128]{2,1,0:T(8,128)S(1)}, f32[1,1]{1,0:T(1,128)}) custom-call(f32[3,64,128]{2,1,0:T(8,128)S(1)} %bitcast.12, f32[3,64,128]{2,1,0:T(8,128)S(1)} %bitcast.13, f32[3,64,128]{2,1,0:T(8,128)S(1)} %bitcast.14, s32[12,64,128]{2,1,0:T(8,128)S(1)} %bitcast.8), custom_call_target="tpu_custom_call" | custom-call | tf_op jit(solution)/shard_map/pallas_call | solution.py:469
  62.4 0.6 copy.12
  63.1 0.6 copy.13
  63.7 0.6 copy.14
Async XLA Ops:
  0.6 1.0 %copy-start = (s32[12,8,8,128]{3,2,1,0:T(8,128)S(1)}, s32[12,8,8,128]{3,2,1,0:T(8,128)}, u32[]{:S(2)}) copy-start(s32[12,8,8,128]{3,2,1,0:T(8,128)} %param.7) | copy-start | bytes 1179652
  1.6 0.9 %copy-start.1 = (f32[3,8,8,128]{3,2,1,0:T(8,128)S(1)}, f32[3,8,8,128]{3,2,1,0:T(8,128)}, u32[]{:S(2)}) copy-start(f32[3,8,8,128]{3,2,1,0:T(8,128)} %param.4) | copy-start | bytes 294916
  2.5 0.9 %copy-start.2 = (f32[3,8,8,128]{3,2,1,0:T(8,128)S(1)}, f32[3,8,8,128]{3,2,1,0:T(8,128)}, u32[]{:S(2)}) copy-start(f32[3,8,8,128]{3,2,1,0:T(8,128)} %param.5) | copy-start | bytes 294916
  3.4 0.9 %copy-start.3 = (f32[3,8,8,128]{3,2,1,0:T(8,128)S(1)}, f32[3,8,8,128]{3,2,1,0:T(8,128)}, u32[]{:S(2)}) copy-start(f32[3,8,8,128]{3,2,1,0:T(8,128)} %param.6) | copy-start | bytes 294916
where the time goes:
time: 66.3 us; the launch traced here: 66.1 us
  Pallas kernels  58.1 us (88%)
  local copies, waits for them, and re-layouts  5.59 us (8%)
  between operations  2.4 us (4%)
    pallas_call x1, Pallas kernels, step(): pl.pallas_call(functools.partial(kernel, sizes), out_shape=(block, block,...  58.1 us
    unnamed x11, local copies, waits for them, and re-layouts  5.59 us

commit v1 on v0

v1 whole, which is shorter than its diff:
```python
import functools
import math

import jax
import jax.numpy as jnp
from jax import lax
from jax.experimental import pallas as pl
from jax.experimental.pallas import tpu as pltpu
from jax.sharding import PartitionSpec as P

MESH = pl.DeviceIdType.MESH
TIME_STEP = 0.05
BITS_PER_WORD = 30
SIDE_X = 4
R = 3
NB = 8
EXT = NB + 2 * R
LANES = 128
REACH = range(-R, R + 1)

FAR = [
    (ez, ex, ey) for ez in (-1, 1) for ex in (0, -1, 1) for ey in (0, -1, 1)
]
NEAR = [(0, ex, ey) for ex in (0, -1, 1) for ey in (0, -1, 1) if (ex, ey) != (0, 0)]
YSLOT = {(ex, ey): i for i, (ex, ey) in enumerate((x, y) for x in (0, -1, 1) for y in (-1, 1))}

CLASSES = {}
for _p in REACH:
    for _r in REACH:
        CLASSES.setdefault(_p * _p + _r * _r, []).append((_p, _r))
CLASSES = sorted(CLASSES.items())


def side(e):
    return 0 if e < 0 else 1


def bond_number(p, q, r):
    flat = (p + R) * 49 + (q + R) * 7 + (r + R)
    return flat if flat < 171 else flat - 1


def weight(p, q, r):
    return 4.0 * math.exp(-(p * p + q * q + r * r) / 9.0)


def kernel(
    sizes,
    disp_hbm,
    vel_hbm,
    body_hbm,
    broken_hbm,
    newd_out,
    newv_out,
    newa_out,
    energy_out,
    disp,
    vel,
    body,
    broken,
    core,
    xpack,
    xrecv,
    ypack,
    yall,
    ynear,
    yfar,
    zrecv,
    zxpack,
    zxrecv,
    yext,
    ext,
    bonds,
    force,
    esum,
    erow,
    eplane,
    ecol,
    load_sem,
    near_send,
    near_recv,
    far_send,
    far_recv,
    esend_sem,
    erecv_sem,
):
    n_gx, n_gy, n_gz = sizes
    gx, gy, gz = lax.axis_index("gx"), lax.axis_index("gy"), lax.axis_index("gz")
    has_low, has_high = gz > 0, gz < n_gz - 1

    def at(ez, ex, ey):
        return (
            lax.rem(gx + ex + n_gx, n_gx),
            lax.rem(gy + ey + n_gy, n_gy),
            gz + ez,
        )

    side_x = SIDE_X
    n_plane = side_x * n_gy * 2
    n_col = (n_gx // side_x) * (n_gz // 2)
    my_x, my_zlo = lax.rem(gx, side_x), gx // side_x
    my_core, my_zhi = lax.rem(gz, 2), gz // 2
    my_plane = (my_x * n_gy + gy) * 2 + my_core
    my_col = my_zhi * (n_gx // side_x) + my_zlo

    def plane_device(m):
        return (
            my_zlo * side_x + m // (2 * n_gy),
            lax.rem(m // 2, n_gy),
            my_zhi * 2 + lax.rem(m, 2),
        )

    def col_device(m):
        return (
            lax.rem(m, n_gx // side_x) * side_x + my_x,
            gy,
            (m // (n_gx // side_x)) * 2 + my_core,
        )

    barrier = pltpu.get_barrier_semaphore()

    def greet(device):
        pl.semaphore_signal(barrier, inc=1, device_id=device, device_id_type=MESH)

    for present, low in ((has_low, True), (has_high, False)):

        @pl.when(present)
        def _(low=low):
            for e in FAR:
                if (e[0] < 0) == low:
                    greet(at(*e))

    for e in NEAR:
        greet(at(*e))

    @pl.loop(1, n_plane)
    def _(j):
        greet(plane_device(lax.rem(my_plane + j, n_plane)))

    @pl.loop(1, n_col)
    def _(j):
        greet(col_device(lax.rem(my_col + j, n_col)))

    loads = [
        pltpu.make_async_copy(src, dst, load_sem.at[i])
        for i, (src, dst) in enumerate(
            ((disp_hbm, disp), (broken_hbm, broken), (vel_hbm, vel), (body_hbm, body))
        )
    ]
    for load in loads:
        load.start()

    lane = lax.broadcasted_iota(jnp.int32, (NB, LANES), 1)
    lane2 = lax.broadcasted_iota(jnp.int32, (2 * NB, LANES), 1)

    for present, low in ((has_low, True), (has_high, False)):

        @pl.when(jnp.logical_not(present))
        def _(low=low):
            s = 0 if low else 1
            for step in (0, 1):
                zrecv[step, s] = jnp.zeros(zrecv.shape[2:], jnp.float32)
                zxrecv[step, s] = jnp.zeros(zxrecv.shape[2:], jnp.float32)
                yfar[step, s] = jnp.zeros(yfar.shape[2:], jnp.float32)

    def near_message(step, e, h):
        _, ex, ey = e
        if ey != 0:
            src = yall.at[0, side(ey)] if step == 0 else ypack.at[h, side(ey)]
            dst = ynear.at[step, YSLOT[ex, ey], h]
        elif step == 0:
            src, dst = xpack.at[0, side(ex)], xrecv.at[0, side(ex)]
        else:
            src, dst = xpack.at[1, side(ex), h], xrecv.at[1, side(ex), h]
        return pltpu.make_async_remote_copy(
            src_ref=src,
            dst_ref=dst,
            send_sem=near_send.at[step, NEAR.index(e), h],
            recv_sem=near_recv.at[step, NEAR.index(e), h],
            device_id=at(0, -ex, -ey),
            device_id_type=MESH,
        )

    def far_message(step, e):
        ez, ex, ey = e
        if ey != 0:
            src = yall.at[step, side(ey)]
            dst = yfar.at[step, side(ez), YSLOT[ex, ey]]
        elif ex == 0:
            src = core.at[step, pl.ds(NB - R if ez < 0 else 0, R)]
            dst = zrecv.at[step, side(ez)]
        else:
            src = zxpack.at[step, side(ez), side(ex)]
            dst = zxrecv.at[step, side(ez), side(ex)]
        return pltpu.make_async_remote_copy(
            src_ref=src,
            dst_ref=dst,
            send_sem=far_send.at[step, FAR.index(e)],
            recv_sem=far_recv.at[step, FAR.index(e)],
            device_id=at(-ez, -ex, -ey),
            device_id_type=MESH,
        )

    def for_far(step, present_below, present_above, act):
        for present, below in ((present_below, True), (present_above, False)):

            @pl.when(present)
            def _(below=below):
                for e in FAR:
                    if (e[0] < 0) == below:
                        act(far_message(step, e))

    def send_far(step):
        for_far(step, has_high, has_low, lambda m: m.start())

    def receive_far(step):
        for_far(step, has_low, has_high, lambda m: m.wait_recv())

    def finish_far(step):
        for_far(step, has_high, has_low, lambda m: m.wait_send())

    def pack_pair(step, h):
        ylow, yhigh = yall[step, 0], yall[step, 1]
        for i, z in enumerate((h, NB - 1 - h)):
            for c in range(3):
                g = 3 * (z * 3 + c)
                k = 3 * (i * 3 + c)
                value = core[step, z, c]
                xpack[step, 0, h, k : k + R, :] = core[step, z, c, NB - R : NB, :]
                xpack[step, 1, h, k : k + R, :] = core[step, z, c, 0:R, :]
                mine = (lane >= g) & (lane < g + R)
                ylow = jnp.where(mine, pltpu.roll(value, g + R, 1), ylow)
                yhigh = jnp.where(mine, pltpu.roll(value, g, 1), yhigh)
        yall[step, 0] = ylow
        yall[step, 1] = yhigh
        if step == 1:
            ypack[h, 0] = ylow
            ypack[h, 1] = yhigh

    def pack_far(step):
        for s, base in ((0, NB - R), (1, 0)):
            for i in range(R):
                for c in range(3):
                    k = 3 * (i * 3 + c)
                    zxpack[step, s, 0, k : k + R, :] = core[
                        step, base + i, c, NB - R : NB, :
                    ]
                    zxpack[step, s, 1, k : k + R, :] = core[step, base + i, c, 0:R, :]

    def shift_row(slot, row, z):
        for c in range(3):
            g = 3 * (z * 3 + c)
            left = pltpu.roll(yext[slot, 0], LANES - R - g, 1)
            right = pltpu.roll(yext[slot, 1], lax.rem(LANES - g, LANES), 1)
            here = ext[R, row, c]
            for r in range(1, R + 1):
                ext[R + r, row, c] = pltpu.roll(
                    jnp.where(lane2 < r, right, here), LANES - r, 1
                )
                ext[R - r, row, c] = pltpu.roll(
                    jnp.where(lane2 >= LANES - r, left, here), r, 1
                )

    def fill_pair(step, h):
        held = 0 if step == 0 else h
        for s, ey in ((0, -1), (1, 1)):
            yext[0, s, R : R + NB, :] = ynear[step, YSLOT[0, ey], held]
            yext[0, s, 0:R, :] = ynear[step, YSLOT[-1, ey], held, NB - R : NB, :]
            yext[0, s, R + NB : EXT, :] = ynear[step, YSLOT[1, ey], held, 0:R, :]
        for i, z in enumerate((h, NB - 1 - h)):
            for c in range(3):
                k = 3 * (i * 3 + c)
                ext[R, z + R, c, R : R + NB, :] = core[step, z, c]
                for s, row in ((0, 0), (1, R + NB)):
                    ext[R, z + R, c, row : row + R, :] = xrecv[
                        step, s, h, k : k + R, :
                    ]
        for z in (h, NB - 1 - h):
            shift_row(0, z + R, z)

    def fill_far(step):
        for zs, first in ((0, 0), (1, R + NB)):
            for i in range(R):
                for c in range(3):
                    k = 3 * (i * 3 + c)
                    ext[R, first + i, c, R : R + NB, :] = zrecv[step, zs, i, c]
                    for s, row in ((0, 0), (1, R + NB)):
                        ext[R, first + i, c, row : row + R, :] = zxrecv[
                            step, zs, s, k : k + R, :
                        ]
            for s, ey in ((0, -1), (1, 1)):
                yext[zs, s, R : R + NB, :] = yfar[step, zs, YSLOT[0, ey]]
                yext[zs, s, 0:R, :] = yfar[step, zs, YSLOT[-1, ey], NB - R : NB, :]
                yext[zs, s, R + NB : EXT, :] = yfar[step, zs, YSLOT[1, ey], 0:R, :]

        @pl.loop(0, R)
        def _(i):
            shift_row(0, i, NB - R + i)
            shift_row(1, R + NB + i, i)

    def unpack_bonds():
        @pl.loop(0, NB)
        def _(z):
            words = [broken[w, pl.ds(z, NB, stride=NB), :] for w in range(12)]
            depth = gz * NB + z
            for q in REACH:
                inside = (depth + q >= 0) & (depth + q < n_gz * NB)
                scale = jnp.where(inside, 1.0, 0.0)
                for _, members in CLASSES:
                    whole = jnp.full(
                        (NB, LANES), scale * weight(members[0][0], q, members[0][1])
                    )
                    for p, r in members:
                        j = (p + R) * 7 + r + R
                        if (p, q, r) == (0, 0, 0):
                            bonds[z, q + R, j] = jnp.zeros((NB, LANES), jnp.float32)
                            continue
                        k = bond_number(p, q, r)
                        bit = words[k // BITS_PER_WORD] & (1 << (k % BITS_PER_WORD))
                        bonds[z, q + R, j] = jnp.where(bit == 0, whole, 0.0)

    def add_row(step, z, q, task):
        cx, cz, cy = (core[step, z, c] for c in range(3))
        cz = cz - q.astype(jnp.float32)
        cxs = {p: cx - float(p) if p else cx for p in REACH}
        cys = {r: cy - float(r) if r else cy for r in REACH}
        row = z + q + R
        fx = fz = fy = energy = None

        def plus(a, b):
            return b if a is None else a + b

        for square, members in CLASSES:
            own = jnp.where(q == 0, 1, 0) if square == 0 else 0
            rest_square = (q * q + square + own).astype(jnp.float32)
            if task != "pull":
                inverse_rest = lax.rsqrt(jnp.full((NB, LANES), rest_square))
            class_energy = None
            for p, r in members:
                there = ext.at[r + R, row]
                j = (p + R) * 7 + r + R
                bx = there[0, R + p : R + p + NB, :] - cxs[p]
                bz = there[1, R + p : R + p + NB, :] - cz
                by = there[2, R + p : R + p + NB, :] - cys[r]
                pull = bonds[z, q + R, j]
                if task != "pull":
                    length_square = bx * bx + bz * bz + by * by
                    if square == 0:
                        length_square = length_square + own.astype(jnp.float32)
                    gap = inverse_rest - lax.rsqrt(length_square)
                    pull = pull * gap
                if task == "energy":
                    bonds[z, q + R, j] = pull
                    class_energy = plus(class_energy, pull * gap * length_square)
                else:
                    fx = plus(fx, pull * bx)
                    fz = plus(fz, pull * bz)
                    fy = plus(fy, pull * by)
            if task == "energy":
                rest = jnp.full((NB, LANES), rest_square) * inverse_rest
                energy = plus(energy, class_energy * rest)
        if task == "energy":
            return energy
        force[step, z, 0] += fx
        force[step, z, 1] += fz
        force[step, z, 2] += fy

    def add_pair(step, z, q, task):
        first = add_row(step, z, q, task)
        second = add_row(step, NB - 1 - z, -q, task)
        if task == "energy":
            esum[...] += first + second

    def phase(turn):
        return lax.rem(turn + NB // 2 - 1, NB // 2)

    loads[0].wait()
    for step in (0, 1):
        yall[step] = jnp.zeros(yall.shape[1:], jnp.float32)
        for s in (0, 1):
            for h in range(NB // 2):
                xpack[step, s, h, 16:24, :] = jnp.zeros((NB, LANES), jnp.float32)
            for t in (0, 1):
                zxpack[step, s, t, 24:32, :] = jnp.zeros((NB, LANES), jnp.float32)

    @pl.loop(0, NB // 2)
    def _(h):
        for z in (h, NB - 1 - h):
            for c in range(3):
                core[0, z, c] = disp[c, pl.ds(z, NB, stride=NB), :]
        pack_pair(0, h)

    pack_far(0)
    half = len(FAR) // 2
    greeted = (
        len(NEAR)
        + half * (jnp.where(has_low, 1, 0) + jnp.where(has_high, 1, 0))
        + (n_plane - 1)
        + (n_col - 1)
    )
    pl.semaphore_wait(barrier, greeted)
    send_far(0)
    for e in NEAR:
        near_message(0, e, 0).start()

    for load in loads[1:]:
        load.wait()
    unpack_bonds()
    esum[...] = jnp.zeros((NB, LANES), jnp.float32)

    @pl.loop(0, NB)
    def _(z):
        for c in range(3):
            value = body[c, pl.ds(z, NB, stride=NB), :]
            force[0, z, c] = value
            force[1, z, c] = value

    for e in NEAR:
        near_message(0, e, 0).wait_recv()

    @pl.loop(0, NB // 2)
    def _(h):
        fill_pair(0, h)

    @pl.loop(0, NB // 2)
    def _(turn):
        h = phase(turn)

        @pl.when(turn == 1)
        def _():
            receive_far(0)
            fill_far(0)

        @pl.loop(0, 2 * R + 1)
        def _(place):
            add_pair(0, h, place - R, "force")

        for z in (h, NB - 1 - h):
            for c in range(3):
                rows = pl.ds(z, NB, stride=NB)
                moved = (
                    core[0, z, c]
                    + TIME_STEP * vel[c, rows, :]
                    + (0.5 * TIME_STEP * TIME_STEP) * force[0, z, c]
                )
                core[1, z, c] = moved
                newd_out[c, rows, :] = moved
        pack_pair(1, h)
        for e in NEAR:
            near_message(1, e, h).start()

    pack_far(1)
    send_far(1)

    @pl.loop(0, NB // 2)
    def _(turn):
        h = phase(turn)
        for e in NEAR:
            near_message(1, e, h).wait_recv()
        fill_pair(1, h)

        @pl.loop(0, h + R + 1)
        def _(z):
            add_pair(1, z, h - z, "energy")

    receive_far(1)
    fill_far(1)

    @pl.loop(1, R + 1)
    def _(q):
        @pl.loop(NB - q, NB)
        def _(z):
            add_pair(1, z, q, "energy")

    erow[0] = jnp.sum(esum[...], axis=0, keepdims=True)
    eplane[my_plane] = erow[0]

    def plane_message(j, slot, device):
        return pltpu.make_async_remote_copy(
            src_ref=erow.at[0],
            dst_ref=eplane.at[slot],
            send_sem=esend_sem.at[0, j],
            recv_sem=erecv_sem.at[0, j],
            device_id=plane_device(device),
            device_id_type=MESH,
        )

    @pl.loop(1, n_plane)
    def _(j):
        plane_message(j, my_plane, lax.rem(my_plane + j, n_plane)).start()

    @pl.loop(0, NB // 2)
    def _(h):
        @pl.loop(0, 2 * R + 1)
        def _(place):
            add_pair(1, h, place - R, "pull")

        for z in (h, NB - 1 - h):
            for c in range(3):
                rows = pl.ds(z, NB, stride=NB)
                newa = force[1, z, c]
                newa_out[c, rows, :] = newa
                newv_out[c, rows, :] = vel[c, rows, :] + (0.5 * TIME_STEP) * (
                    force[0, z, c] + newa
                )

    @pl.loop(1, n_plane)
    def _(j):
        other = lax.rem(my_plane - j + n_plane, n_plane)
        plane_message(j, other, other).wait()

    total = eplane[0]
    for m in range(1, n_plane):
        total = total + eplane[m]
    erow[1] = total
    ecol[my_col] = total

    def col_message(j, slot, device):
        return pltpu.make_async_remote_copy(
            src_ref=erow.at[1],
            dst_ref=ecol.at[slot],
            send_sem=esend_sem.at[1, j],
            recv_sem=erecv_sem.at[1, j],
            device_id=col_device(device),
            device_id_type=MESH,
        )

    @pl.loop(1, n_col)
    def _(j):
        col_message(j, my_col, lax.rem(my_col + j, n_col)).start()

    for e in NEAR:
        near_message(0, e, 0).wait_send()

    @pl.loop(0, NB // 2)
    def _(h):
        for e in NEAR:
            near_message(1, e, h).wait_send()

    finish_far(0)
    finish_far(1)

    @pl.loop(1, n_col)
    def _(j):
        other = lax.rem(my_col - j + n_col, n_col)
        col_message(j, other, other).wait()

    total = ecol[0]
    for m in range(1, n_col):
        total = total + ecol[m]
    area = (n_gx * NB) * (n_gy * LANES)
    energy_out[0, 0] = jnp.sum(total) * (0.25 / area)


def solution(mesh):
    sizes = (mesh.shape["gx"], mesh.shape["gy"], mesh.shape["gz"])
    f32 = jnp.float32
    block = jax.ShapeDtypeStruct((3, NB * NB, LANES), f32)

    def step(displacement, velocity, body_force, broken):
        flat = [
            a.reshape(a.shape[0], NB * NB, LANES)
            for a in (displacement, velocity, body_force, broken)
        ]
        newd, newv, newa, energy = pl.pallas_call(
            functools.partial(kernel, sizes),
            out_shape=(block, block, block, jax.ShapeDtypeStruct((1, 1), f32)),
            in_specs=[pl.BlockSpec(memory_space=pl.ANY)] * 4,
            out_specs=[pl.BlockSpec(memory_space=pltpu.VMEM)] * 3
            + [pl.BlockSpec(memory_space=pltpu.SMEM)],
            scratch_shapes=[
                pltpu.VMEM((3, NB * NB, LANES), f32),
                pltpu.VMEM((3, NB * NB, LANES), f32),
                pltpu.VMEM((3, NB * NB, LANES), f32),
                pltpu.VMEM((12, NB * NB, LANES), jnp.int32),
                pltpu.VMEM((2, NB, 3, NB, LANES), f32),
                pltpu.VMEM((2, 2, NB // 2, 24, LANES), f32),
                pltpu.VMEM((2, 2, NB // 2, 24, LANES), f32),
                pltpu.VMEM((NB // 2, 2, NB, LANES), f32),
                pltpu.VMEM((2, 2, NB, LANES), f32),
                pltpu.VMEM((2, 6, NB // 2, NB, LANES), f32),
                pltpu.VMEM((2, 2, 6, NB, LANES), f32),
                pltpu.VMEM((2, 2, R, 3, NB, LANES), f32),
                pltpu.VMEM((2, 2, 2, 32, LANES), f32),
                pltpu.VMEM((2, 2, 2, 32, LANES), f32),
                pltpu.VMEM((2, 2, 2 * NB, LANES), f32),
                pltpu.VMEM((7, EXT, 3, 2 * NB, LANES), f32),
                pltpu.VMEM((NB, 7, 49, NB, LANES), f32),
                pltpu.VMEM((2, NB, 3, NB, LANES), f32),
                pltpu.VMEM((NB, LANES), f32),
                pltpu.VMEM((2, 1, LANES), f32),
                pltpu.VMEM((32, 1, LANES), f32),
                pltpu.VMEM((8, 1, LANES), f32),
                pltpu.SemaphoreType.DMA((4,)),
                pltpu.SemaphoreType.DMA((2, len(NEAR), NB // 2)),
                pltpu.SemaphoreType.DMA((2, len(NEAR), NB // 2)),
                pltpu.SemaphoreType.DMA((2, len(FAR))),
                pltpu.SemaphoreType.DMA((2, len(FAR))),
                pltpu.SemaphoreType.DMA((2, 32)),
                pltpu.SemaphoreType.DMA((2, 32)),
            ],
            compiler_params=pltpu.CompilerParams(
                collective_id=0,
                has_side_effects=True,
                vmem_limit_bytes=66_700_000,
            ),
        )(*flat)
        shape = displacement.shape
        return (
            newd.reshape(shape),
            newv.reshape(shape),
            newa.reshape(shape),
            energy.reshape(()),
        )

    spec = P(None, "gx", "gz", "gy")
    return jax.shard_map(
        step,
        mesh=mesh,
        in_specs=(spec,) * 4,
        out_specs=(spec,) * 3 + (P(),),
        check_vma=False,
    )
```

time: 66.3 us -> 57.5 us (0.87)
  Pallas kernels: 58.1 us -> 51.3 us
  local copies, waits for them, and re-layouts: 5.59 us -> 3.15 us
    pallas_call x1, Pallas kernels: 58.1 us -> 51.3 us  [step(): pl.pallas_call(functools.partial(kernel, sizes), out_shape=(block, block,...]
    unnamed x11 -> x7, local copies, waits for them, and re-layouts: 5.59 us -> 3.15 us
where the time goes in v1:
time: 57.5 us; the launch traced here: 56.8 us
  Pallas kernels  51.3 us (89%)
  local copies, waits for them, and re-layouts  3.15 us (5%)
  between operations  2.34 us (4%)
    pallas_call x1, Pallas kernels, step(): pl.pallas_call(functools.partial(kernel, sizes), out_shape=(block, block,...  51.3 us
    unnamed x7, local copies, waits for them, and re-layouts  3.15 us

profile of v1, /device:TPU:1, one launch (start us, length us, event | category | flops | bytes accessed | tf_op | source)
XLA Modules:
  0.0 56.8 jit_solution(16589911591014809493)
XLA Ops:
  0.6 51.3 %shard_map.75 = (f32[3,64,128]{2,1,0:T(8,128)}, f32[3,64,128]{2,1,0:T(8,128)}, f32[3,64,128]{2,1,0:T(8,128)}, f32[1,1]{1,0:T(1,128)}) custom-call(f32[3,64,128]{2,1,0:T(8,128)} %bitcast.12, f32[3,64,128]{2,1,0:T(8,128)} %bitcast.13, f32[3,64,128]{2,1,0:T(8,128)} %bitcast.14, s32[12,64,128]{2,1,0:T(8,128)} %bitcast.8), custom_call_target="tpu_custom_call" | custom-call | tf_op jit(solution)/shard_map/pallas_call | solution.py:565
  51.9 0.0 copy-start.1
  51.9 1.6 %copy.12 = f32[3,8,8,128]{3,2,1,0:T(8,128)} copy(f32[3,8,8,128]{3,2,1,0:T(8,128)} %bitcast.11) | data formatting | bytes 196608
  53.5 0.0 copy-done.1
  53.5 0.0 copy-start
  53.5 0.6 %copy.13 = f32[3,8,8,128]{3,2,1,0:T(8,128)} copy(f32[3,8,8,128]{3,2,1,0:T(8,128)S(1)} %bitcast.10) | data formatting | bytes 196608
  54.1 0.3 copy-done
  54.4 0.6 %copy.14 = f32[3,8,8,128]{3,2,1,0:T(8,128)} copy(f32[3,8,8,128]{3,2,1,0:T(8,128)S(1)} %bitcast.9) | data formatting | bytes 196608
Async XLA Ops:
  51.9 1.6 %copy-start.1 = (f32[3,64,128]{2,1,0:T(8,128)S(1)}, f32[3,64,128]{2,1,0:T(8,128)}, u32[]{:S(2)}) copy-start(f32[3,64,128]{2,1,0:T(8,128)} %get-tuple-element.9) | copy-start | bytes 294916
  53.5 0.9 %copy-start = (f32[3,64,128]{2,1,0:T(8,128)S(1)}, f32[3,64,128]{2,1,0:T(8,128)}, u32[]{:S(2)}) copy-start(f32[3,64,128]{2,1,0:T(8,128)} %get-tuple-element.10) | copy-start | bytes 294916

commit v2 on v1

--- a/solution.py
+++ b/solution.py
@@ -152,6 +152,11 @@
 
     lane = lax.broadcasted_iota(jnp.int32, (NB, LANES), 1)
     lane2 = lax.broadcasted_iota(jnp.int32, (2 * NB, LANES), 1)
+    middle = 0.5 * (NB - 1)
+    place = lax.broadcasted_iota(jnp.int32, (NB, LANES), 0).astype(jnp.float32) - middle
+    place2 = lax.broadcasted_iota(jnp.int32, (2 * NB, LANES), 0).astype(
+        jnp.float32
+    ) - (middle + R)
 
     for present, low in ((has_low, True), (has_high, False)):
 
@@ -247,19 +252,29 @@
                     ]
                     zxpack[step, s, 1, k : k + R, :] = core[step, base + i, c, 0:R, :]
 
-    def shift_row(slot, row, z):
-        for c in range(3):
-            g = 3 * (z * 3 + c)
-            left = pltpu.roll(yext[slot, 0], LANES - R - g, 1)
-            right = pltpu.roll(yext[slot, 1], lax.rem(LANES - g, LANES), 1)
-            here = ext[R, row, c]
-            for r in range(1, R + 1):
-                ext[R + r, row, c] = pltpu.roll(
-                    jnp.where(lane2 < r, right, here), LANES - r, 1
-                )
-                ext[R - r, row, c] = pltpu.roll(
-                    jnp.where(lane2 >= LANES - r, left, here), r, 1
-                )
+    def shift_rows(rows):
+        strips = {slot: (yext[slot, 0], yext[slot, 1]) for slot, _, _ in rows}
+        here = [[ext[R, row, c] for c in range(3)] for _, row, _ in rows]
+        for (slot, row, z), values in zip(rows, here):
+            for c in range(3):
+                g = 3 * (z * 3 + c)
+                left = pltpu.roll(strips[slot][0], LANES - R - g, 1)
+                right = pltpu.roll(strips[slot][1], lax.rem(LANES - g, LANES), 1)
+                value = values[c]
+                if c == 0:
+                    left, right, value = left + place2, right + place2, value + place2
+                    ext[R, row, c] = value
+                for r in range(1, R + 1):
+                    after = pltpu.roll(
+                        jnp.where(lane2 < r, right, value), LANES - r, 1
+                    )
+                    before = pltpu.roll(
+                        jnp.where(lane2 >= LANES - r, left, value), r, 1
+                    )
+                    if c == 2:
+                        after, before = after + float(r), before - float(r)
+                    ext[R + r, row, c] = after
+                    ext[R - r, row, c] = before
 
     def fill_pair(step, h):
         held = 0 if step == 0 else h
@@ -275,8 +290,7 @@
                     ext[R, z + R, c, row : row + R, :] = xrecv[
                         step, s, h, k : k + R, :
                     ]
-        for z in (h, NB - 1 - h):
-            shift_row(0, z + R, z)
+        shift_rows([(0, z + R, z) for z in (h, NB - 1 - h)])
 
     def fill_far(step):
         for zs, first in ((0, 0), (1, R + NB)):
@@ -295,8 +309,7 @@
 
         @pl.loop(0, R)
         def _(i):
-            shift_row(0, i, NB - R + i)
-            shift_row(1, R + NB + i, i)
+            shift_rows([(0, i, NB - R + i), (1, R + NB + i, i)])
 
     def unpack_bonds():
         @pl.loop(0, NB)
@@ -321,9 +334,8 @@
 
     def add_row(step, z, q, task):
         cx, cz, cy = (core[step, z, c] for c in range(3))
+        cx = cx + place
         cz = cz - q.astype(jnp.float32)
-        cxs = {p: cx - float(p) if p else cx for p in REACH}
-        cys = {r: cy - float(r) if r else cy for r in REACH}
         row = z + q + R
         fx = fz = fy = energy = None
 
@@ -339,9 +351,9 @@
             for p, r in members:
                 there = ext.at[r + R, row]
                 j = (p + R) * 7 + r + R
-                bx = there[0, R + p : R + p + NB, :] - cxs[p]
+                bx = there[0, R + p : R + p + NB, :] - cx
                 bz = there[1, R + p : R + p + NB, :] - cz
-                by = there[2, R + p : R + p + NB, :] - cys[r]
+                by = there[2, R + p : R + p + NB, :] - cy
                 pull = bonds[z, q + R, j]
                 if task != "pull":
                     length_square = bx * bx + bz * bz + by * by
@@ -432,8 +444,8 @@
             fill_far(0)
 
         @pl.loop(0, 2 * R + 1)
-        def _(place):
-            add_pair(0, h, place - R, "force")
+        def _(step_q):
+            add_pair(0, h, step_q - R, "force")
 
         for z in (h, NB - 1 - h):
             for c in range(3):
@@ -492,8 +504,8 @@
     @pl.loop(0, NB // 2)
     def _(h):
         @pl.loop(0, 2 * R + 1)
-        def _(place):
-            add_pair(1, h, place - R, "pull")
+        def _(step_q):
+            add_pair(1, h, step_q - R, "pull")
 
         for z in (h, NB - 1 - h):
             for c in range(3):
@@ -550,6 +562,17 @@
         total = total + ecol[m]
     area = (n_gx * NB) * (n_gy * LANES)
     energy_out[0, 0] = jnp.sum(total) * (0.25 / area)
+
+
+def hand_out(*refs):
+    n = len(refs) // 2
+    copies = [
+        pltpu.make_async_copy(refs[i], refs[n + i], refs[2 * n].at[i]) for i in range(n)
+    ]
+    for copy in copies:
+        copy.start()
+    for copy in copies:
+        copy.wait()
 
 
 def solution(mesh):
@@ -602,9 +625,17 @@
             compiler_params=pltpu.CompilerParams(
                 collective_id=0,
                 has_side_effects=True,
-                vmem_limit_bytes=66_700_000,
+                vmem_limit_bytes=40_000_000,
             ),
-        )(*flat)
+        )(*[pltpu.with_memory_space_constraint(a, pltpu.HBM) for a in flat])
+        newd, newv, newa = pl.pallas_call(
+            hand_out,
+            out_shape=(block,) * 3,
+            in_specs=[pl.BlockSpec(memory_space=pl.ANY)] * 3,
+            out_specs=[pl.BlockSpec(memory_space=pl.ANY)] * 3,
+            scratch_shapes=[pltpu.SemaphoreType.DMA((3,))],
+            compiler_params=pltpu.CompilerParams(vmem_limit_bytes=40_000_000),
+        )(newd, newv, newa)
         shape = displacement.shape
         return (
             newd.reshape(shape),

time: 57.5 us -> 54.5 us (0.948)
  local copies, waits for them, and re-layouts: 3.15 us -> 0 us
    unnamed x7 -> x0, local copies, waits for them, and re-layouts: 3.15 us -> none
    pallas_call x0 -> x1, Pallas kernels: none -> 0.73 us  [step(): pl.pallas_call(hand_out, out_shape=(block,) * 3, in_specs=[pl.BlockSpec(m...]
where the time goes in v2:
time: 54.5 us; the launch traced here: 54 us
  Pallas kernels  51.6 us (95%)
  between operations  2.4 us (4%)
    pallas_call x1, Pallas kernels, step(): pl.pallas_call(functools.partial(kernel, sizes), out_shape=(block, block,...  50.9 us

profile of v2, /device:TPU:1, one launch (start us, length us, event | category | flops | bytes accessed | tf_op | source)
XLA Modules:
  0.0 54.0 jit_solution(13311389198428686665)
XLA Ops:
  0.6 50.9 %shard_map.75 = (f32[3,64,128]{2,1,0:T(8,128)S(1)}, f32[3,64,128]{2,1,0:T(8,128)S(1)}, f32[3,64,128]{2,1,0:T(8,128)S(1)}, f32[1,1]{1,0:T(1,128)}) custom-call(f32[3,64,128]{2,1,0:T(8,128)} %bitcast.9, f32[3,64,128]{2,1,0:T(8,128)} %bitcast.10, f32[3,64,128]{2,1,0:T(8,128)} %bitcast.11, s32[12,64,128]{2,1,0:T(8,128)} %bitcast.8), custom_call_target="tpu_custom_call" | custom-call | tf_op jit(solution)/shard_map/pallas_call | solution.py:588
  51.5 0.7 %shard_map.76 = (f32[3,64,128]{2,1,0:T(8,128)}, f32[3,64,128]{2,1,0:T(8,128)}, f32[3,64,128]{2,1,0:T(8,128)}) custom-call(f32[3,64,128]{2,1,0:T(8,128)S(1)} %get-tuple-element.11.refs_0_, f32[3,64,128]{2,1,0:T(8,128)S(1)} %get-tuple-element.12.refs_1_, f32[3,64,128]{2,1,0:T(8,128)S(1)} %get-tuple-element.13.refs_2_), custom_call_target="tpu_custom_call" | custom-call | tf_op jit(solution)/shard_map/pallas_call | solution.py:631

commit v3 on v2

--- a/solution.py
+++ b/solution.py
@@ -95,51 +95,34 @@
             gz + ez,
         )
 
-    side_x = SIDE_X
-    n_plane = side_x * n_gy * 2
-    n_col = (n_gx // side_x) * (n_gz // 2)
-    my_x, my_zlo = lax.rem(gx, side_x), gx // side_x
-    my_core, my_zhi = lax.rem(gz, 2), gz // 2
-    my_plane = (my_x * n_gy + gy) * 2 + my_core
-    my_col = my_zhi * (n_gx // side_x) + my_zlo
-
-    def plane_device(m):
-        return (
-            my_zlo * side_x + m // (2 * n_gy),
-            lax.rem(m // 2, n_gy),
-            my_zhi * 2 + lax.rem(m, 2),
-        )
-
-    def col_device(m):
-        return (
-            lax.rem(m, n_gx // side_x) * side_x + my_x,
-            gy,
-            (m // (n_gx // side_x)) * 2 + my_core,
-        )
-
-    barrier = pltpu.get_barrier_semaphore()
-
-    def greet(device):
-        pl.semaphore_signal(barrier, inc=1, device_id=device, device_id_type=MESH)
-
-    for present, low in ((has_low, True), (has_high, False)):
-
-        @pl.when(present)
-        def _(low=low):
-            for e in FAR:
-                if (e[0] < 0) == low:
-                    greet(at(*e))
-
-    for e in NEAR:
-        greet(at(*e))
-
-    @pl.loop(1, n_plane)
-    def _(j):
-        greet(plane_device(lax.rem(my_plane + j, n_plane)))
-
-    @pl.loop(1, n_col)
-    def _(j):
-        greet(col_device(lax.rem(my_col + j, n_col)))
+    n_zlo, n_zhi = n_gx // SIDE_X, n_gz // 2
+    xs = [lax.rem(gx + d, SIDE_X) for d in range(SIDE_X)]
+    ys = [lax.rem(gy + d, n_gy) for d in range(n_gy)]
+    cores = [lax.rem(gz + d, 2) for d in range(2)]
+    lows = [lax.rem(gx // SIDE_X + d, n_zlo) for d in range(n_zlo)]
+    highs = [lax.rem(gz // 2 + d, n_zhi) for d in range(n_zhi)]
+    plane = [
+        (x, y, c) for x in range(SIDE_X) for y in range(n_gy) for c in range(2)
+    ]
+    column = [(0, 0, 0, h, l) for h in range(n_zhi) for l in range(n_zlo)]
+    stages = (
+        [(x, y, c, 0, 0) for x, y, c in plane],
+        column,
+    )
+
+    def partner(d):
+        x, y, c, h, l = d
+        return lows[l] * SIDE_X + xs[x], ys[y], highs[h] * 2 + cores[c]
+
+    def place_of(stage, d):
+        x, y, c, h, l = d
+        if stage == 0:
+            return (xs[x] * n_gy + ys[y]) * 2 + cores[c]
+        return highs[h] * n_zlo + lows[l]
+
+    def opposite(d):
+        sizes = (SIDE_X, n_gy, 2, n_zhi, n_zlo)
+        return tuple((n - k) % n for k, n in zip(d, sizes))
 
     loads = [
         pltpu.make_async_copy(src, dst, load_sem.at[i])
@@ -149,6 +132,26 @@
     ]
     for load in loads:
         load.start()
+
+    barrier = pltpu.get_barrier_semaphore()
+
+    def greet(device):
+        pl.semaphore_signal(barrier, inc=1, device_id=device, device_id_type=MESH)
+
+    for present, low in ((has_low, True), (has_high, False)):
+
+        @pl.when(present)
+        def _(low=low):
+            for e in FAR:
+                if (e[0] < 0) == low:
+                    greet(at(*e))
+
+    for e in NEAR:
+        greet(at(*e))
+
+    for stage in stages:
+        for d in stage[1:]:
+            greet(partner(d))
 
     lane = lax.broadcasted_iota(jnp.int32, (NB, LANES), 1)
     lane2 = lax.broadcasted_iota(jnp.int32, (2 * NB, LANES), 1)
@@ -348,6 +351,7 @@
             if task != "pull":
                 inverse_rest = lax.rsqrt(jnp.full((NB, LANES), rest_square))
             class_energy = None
+            cf = [None] * 3
             for p, r in members:
                 there = ext.at[r + R, row]
                 j = (p + R) * 7 + r + R
@@ -365,9 +369,9 @@
                     bonds[z, q + R, j] = pull
                     class_energy = plus(class_energy, pull * gap * length_square)
                 else:
-                    fx = plus(fx, pull * bx)
-                    fz = plus(fz, pull * bz)
-                    fy = plus(fy, pull * by)
+                    cf = [plus(a, pull * b) for a, b in zip(cf, (bx, bz, by))]
+            if task != "energy":
+                fx, fz, fy = plus(fx, cf[0]), plus(fz, cf[1]), plus(fy, cf[2])
             if task == "energy":
                 rest = jnp.full((NB, LANES), rest_square) * inverse_rest
                 energy = plus(energy, class_energy * rest)
@@ -407,8 +411,8 @@
     greeted = (
         len(NEAR)
         + half * (jnp.where(has_low, 1, 0) + jnp.where(has_high, 1, 0))
-        + (n_plane - 1)
-        + (n_col - 1)
+        + len(stages[0] + stages[1])
+        - 2
     )
     pl.semaphore_wait(barrier, greeted)
     send_far(0)
@@ -484,28 +488,40 @@
         def _(z):
             add_pair(1, z, q, "energy")
 
-    erow[0] = jnp.sum(esum[...], axis=0, keepdims=True)
-    eplane[my_plane] = erow[0]
-
-    def plane_message(j, slot, device):
+    def energy_message(stage, i, sender):
+        gathered = (eplane, ecol)[stage]
         return pltpu.make_async_remote_copy(
-            src_ref=erow.at[0],
-            dst_ref=eplane.at[slot],
-            send_sem=esend_sem.at[0, j],
-            recv_sem=erecv_sem.at[0, j],
-            device_id=plane_device(device),
+            src_ref=erow.at[stage],
+            dst_ref=gathered.at[place_of(stage, sender)],
+            send_sem=esend_sem.at[stage, i],
+            recv_sem=erecv_sem.at[stage, i],
+            device_id=partner(stages[stage][i]),
             device_id_type=MESH,
         )
 
-    @pl.loop(1, n_plane)
-    def _(j):
-        plane_message(j, my_plane, lax.rem(my_plane + j, n_plane)).start()
+    def spread(stage, row):
+        me = stages[stage][0]
+        erow[stage] = row
+        (eplane, ecol)[stage][place_of(stage, me)] = row
+        for i in range(1, len(stages[stage])):
+            energy_message(stage, i, me).start()
+
+    def gather(stage):
+        gathered, count = (eplane, ecol)[stage], len(stages[stage])
+        for i in range(1, count):
+            energy_message(stage, i, opposite(stages[stage][i])).wait()
+        rows = [gathered[m] for m in range(count)]
+        while len(rows) > 1:
+            rows = [a + b for a, b in zip(rows[::2], rows[1::2])]
+        return rows[0]
+
+    spread(0, jnp.sum(esum[...], axis=0, keepdims=True))
 
     @pl.loop(0, NB // 2)
     def _(h):
         @pl.loop(0, 2 * R + 1)
-        def _(step_q):
-            add_pair(1, h, step_q - R, "pull")
+        def _(t):
+            add_pair(1, h, t - R, "pull")
 
         for z in (h, NB - 1 - h):
             for c in range(3):
@@ -516,30 +532,7 @@
                     force[0, z, c] + newa
                 )
 
-    @pl.loop(1, n_plane)
-    def _(j):
-        other = lax.rem(my_plane - j + n_plane, n_plane)
-        plane_message(j, other, other).wait()
-
-    total = eplane[0]
-    for m in range(1, n_plane):
-        total = total + eplane[m]
-    erow[1] = total
-    ecol[my_col] = total
-
-    def col_message(j, slot, device):
-        return pltpu.make_async_remote_copy(
-            src_ref=erow.at[1],
-            dst_ref=ecol.at[slot],
-            send_sem=esend_sem.at[1, j],
-            recv_sem=erecv_sem.at[1, j],
-            device_id=col_device(device),
-            device_id_type=MESH,
-        )
-
-    @pl.loop(1, n_col)
-    def _(j):
-        col_message(j, my_col, lax.rem(my_col + j, n_col)).start()
+    spread(1, gather(0))
 
     for e in NEAR:
         near_message(0, e, 0).wait_send()
@@ -551,15 +544,7 @@
 
     finish_far(0)
     finish_far(1)
-
-    @pl.loop(1, n_col)
-    def _(j):
-        other = lax.rem(my_col - j + n_col, n_col)
-        col_message(j, other, other).wait()
-
-    total = ecol[0]
-    for m in range(1, n_col):
-        total = total + ecol[m]
+    total = gather(1)
     area = (n_gx * NB) * (n_gy * LANES)
     energy_out[0, 0] = jnp.sum(total) * (0.25 / area)
 

time: 54.5 us -> 52.9 us (0.971)
  Pallas kernels: 51.6 us -> 50.4 us
    pallas_call x1, Pallas kernels: 50.9 us -> 49.7 us  [step(): pl.pallas_call(functools.partial(kernel, sizes), out_shape=(block, block,...]
where the time goes in v3:
time: 52.9 us; the launch traced here: 52.8 us
  Pallas kernels  50.4 us (95%)
  between operations  2.4 us (5%)
    pallas_call x1, Pallas kernels, step(): pl.pallas_call(functools.partial(kernel, sizes), out_shape=(block, block,...  49.7 us

profile of v3, /device:TPU:1, one launch (start us, length us, event | category | flops | bytes accessed | tf_op | source)
XLA Modules:
  0.0 52.8 jit_solution(4472260385929284821)
XLA Ops:
  0.6 49.7 %shard_map.75 = (f32[3,64,128]{2,1,0:T(8,128)S(1)}, f32[3,64,128]{2,1,0:T(8,128)S(1)}, f32[3,64,128]{2,1,0:T(8,128)S(1)}, f32[1,1]{1,0:T(1,128)}) custom-call(f32[3,64,128]{2,1,0:T(8,128)} %bitcast.9, f32[3,64,128]{2,1,0:T(8,128)} %bitcast.10, f32[3,64,128]{2,1,0:T(8,128)} %bitcast.11, s32[12,64,128]{2,1,0:T(8,128)} %bitcast.8), custom_call_target="tpu_custom_call" | custom-call | tf_op jit(solution)/shard_map/pallas_call | solution.py:573
  50.3 0.7 %shard_map.76 = (f32[3,64,128]{2,1,0:T(8,128)}, f32[3,64,128]{2,1,0:T(8,128)}, f32[3,64,128]{2,1,0:T(8,128)}) custom-call(f32[3,64,128]{2,1,0:T(8,128)S(1)} %get-tuple-element.11.refs_0_, f32[3,64,128]{2,1,0:T(8,128)S(1)} %get-tuple-element.12.refs_1_, f32[3,64,128]{2,1,0:T(8,128)S(1)} %get-tuple-element.13.refs_2_), custom_call_target="tpu_custom_call" | custom-call | tf_op jit(solution)/shard_map/pallas_call | solution.py:616

commit v4 on v3

--- a/solution.py
+++ b/solution.py
@@ -81,6 +81,8 @@
     near_recv,
     far_send,
     far_recv,
+    early_send,
+    early_recv,
     esend_sem,
     erecv_sem,
 ):
@@ -189,14 +191,26 @@
             device_id_type=MESH,
         )
 
+    def early_message(ez):
+        e = (ez, 0, 0)
+        return pltpu.make_async_remote_copy(
+            src_ref=core.at[1, pl.ds(NB - R + 1 if ez < 0 else 0, R - 1)],
+            dst_ref=zrecv.at[1, side(ez), pl.ds(1 if ez < 0 else 0, R - 1)],
+            send_sem=early_send.at[side(ez)],
+            recv_sem=early_recv.at[side(ez)],
+            device_id=at(-ez, 0, 0),
+            device_id_type=MESH,
+        )
+
     def far_message(step, e):
         ez, ex, ey = e
         if ey != 0:
             src = yall.at[step, side(ey)]
             dst = yfar.at[step, side(ez), YSLOT[ex, ey]]
         elif ex == 0:
-            src = core.at[step, pl.ds(NB - R if ez < 0 else 0, R)]
-            dst = zrecv.at[step, side(ez)]
+            first, count = (0, R) if step == 0 else (0 if ez < 0 else R - 1, 1)
+            src = core.at[step, pl.ds((NB - R if ez < 0 else 0) + first, count)]
+            dst = zrecv.at[step, side(ez), pl.ds(first, count)]
         else:
             src = zxpack.at[step, side(ez), side(ex)]
             dst = zxrecv.at[step, side(ez), side(ex)]
@@ -218,14 +232,25 @@
                     if (e[0] < 0) == below:
                         act(far_message(step, e))
 
+    def for_early(present_below, present_above, act):
+        for present, ez in ((present_below, -1), (present_above, 1)):
+
+            @pl.when(present)
+            def _(ez=ez):
+                act(early_message(ez))
+
     def send_far(step):
         for_far(step, has_high, has_low, lambda m: m.start())
 
     def receive_far(step):
         for_far(step, has_low, has_high, lambda m: m.wait_recv())
+        if step == 1:
+            for_early(has_low, has_high, lambda m: m.wait_recv())
 
     def finish_far(step):
         for_far(step, has_high, has_low, lambda m: m.wait_send())
+        if step == 1:
+            for_early(has_high, has_low, lambda m: m.wait_send())
 
     def pack_pair(step, h):
         ylow, yhigh = yall[step, 0], yall[step, 1]
@@ -464,6 +489,10 @@
         pack_pair(1, h)
         for e in NEAR:
             near_message(1, e, h).start()
+
+        @pl.when(turn == R - 1)
+        def _():
+            for_early(has_high, has_low, lambda m: m.start())
 
     pack_far(1)
     send_far(1)
@@ -604,6 +633,8 @@
                 pltpu.SemaphoreType.DMA((2, len(NEAR), NB // 2)),
                 pltpu.SemaphoreType.DMA((2, len(FAR))),
                 pltpu.SemaphoreType.DMA((2, len(FAR))),
+                pltpu.SemaphoreType.DMA((2,)),
+                pltpu.SemaphoreType.DMA((2,)),
                 pltpu.SemaphoreType.DMA((2, 32)),
                 pltpu.SemaphoreType.DMA((2, 32)),
             ],

time: 52.9 us -> 52.3 us (0.989)
  Pallas kernels: 50.4 us -> 49.8 us
    pallas_call x1, Pallas kernels: 49.7 us -> 49.1 us  [step(): pl.pallas_call(functools.partial(kernel, sizes), out_shape=(block, block,...]
where the time goes in v4:
time: 52.3 us; the launch traced here: 52.2 us
  Pallas kernels  49.8 us (95%)
  between operations  2.4 us (5%)
    pallas_call x1, Pallas kernels, step(): pl.pallas_call(functools.partial(kernel, sizes), out_shape=(block, block,...  49.1 us

profile of v4, /device:TPU:1, one launch (start us, length us, event | category | flops | bytes accessed | tf_op | source)
XLA Modules:
  0.0 52.2 jit_solution(15147222188825034112)
XLA Ops:
  0.6 49.1 %shard_map.75 = (f32[3,64,128]{2,1,0:T(8,128)S(1)}, f32[3,64,128]{2,1,0:T(8,128)S(1)}, f32[3,64,128]{2,1,0:T(8,128)S(1)}, f32[1,1]{1,0:T(1,128)}) custom-call(f32[3,64,128]{2,1,0:T(8,128)} %bitcast.9, f32[3,64,128]{2,1,0:T(8,128)} %bitcast.10, f32[3,64,128]{2,1,0:T(8,128)} %bitcast.11, s32[12,64,128]{2,1,0:T(8,128)} %bitcast.8), custom_call_target="tpu_custom_call" | custom-call | tf_op jit(solution)/shard_map/pallas_call | solution.py:602
  49.7 0.7 %shard_map.76 = (f32[3,64,128]{2,1,0:T(8,128)}, f32[3,64,128]{2,1,0:T(8,128)}, f32[3,64,128]{2,1,0:T(8,128)}) custom-call(f32[3,64,128]{2,1,0:T(8,128)S(1)} %get-tuple-element.11.refs_0_, f32[3,64,128]{2,1,0:T(8,128)S(1)} %get-tuple-element.12.refs_1_, f32[3,64,128]{2,1,0:T(8,128)S(1)} %get-tuple-element.13.refs_2_), custom_call_target="tpu_custom_call" | custom-call | tf_op jit(solution)/shard_map/pallas_call | solution.py:647
